TPU v7x, 512 devices: a whole 4x8x8 slice. The times are simulated.
512 devices in a mesh: frame: 32 (over y_lo, z, core), space: 16 (over x, y_hi).
Axes of the slice: x: 4, y: 8 (y_hi: 4, y_lo: 2; y = y_hi * 2 + y_lo), z: 8, core: 2. Of those that a mesh axis runs over, the one named last changes fastest.
Arguments:
- spatial_query: bfloat16 [32, 1024, 1152], P('frame', 'space'), may hold values from -24 to 24
- spatial_key: bfloat16 [32, 1024, 1152], P('frame', 'space'), may hold values from -24 to 24
- spatial_value: bfloat16 [32, 1024, 1152], P('frame', 'space'), may hold values from -6 to 6
- latents: bfloat16 [32, 1024, 1152], P('frame', 'space'), may hold values from -6 to 6
- proj_weight: bfloat16 [1152, 1152], P('frame'), may hold values from -0.1875 to 0.1875
- proj_bias: float32 [1152], replicated, may hold values from -3 to 3
- residual_gate: float32 [1152], replicated, may hold values from 0.5 to 1.5
- temporal_shift: float32 [1152], replicated, may hold values from -3 to 3
- temporal_scale: float32 [1152], replicated, may hold values from -0.5 to 0.5
- temporal_weight: bfloat16 [1152, 3456], P('frame'), may hold values from -0.75 to 0.75
- clip_lengths: int32 [16], replicated, may hold values from 1 to 4, 32 in all
Outputs:
- hidden: float32 [32, 1024, 1152], P('frame', 'space')
- temporal_out: float32 [32, 1024, 1152], P('frame', 'space')
Inputs may be any that keep to these rules, and one draw needn't show every extreme that they name: `clip_lengths`: 16 clips fill the 32 frames in order; one clip has exactly 4 frames.
All inputs are finite; a program needn't handle non-finite values.
Results may differ from a plain program's by a relative error of at most 0.012.
Values may be sent and summed in bfloat16 or wider, within the bound.
A program may use at most 64 MiB of HBM per device.

v0:
```python
import math
import jax
import jax.numpy as jnp
from jax import lax
from jax.sharding import Mesh
from jax.sharding import PartitionSpec as P

HEADS = 16
FRAME = ("frame_0", "frame_1", "frame_2")
neg_fill = -1e30


def in_blocks(shard, dim, devices):
    before, after = (shard.shape[:dim], shard.shape[dim + 1 :])
    return jnp.moveaxis(shard.reshape(*before, devices, -1, *after), dim, 0)


def in_order(blocks, dim):
    shape = list(blocks.shape[1:])
    shape[dim] *= blocks.shape[0]
    return jnp.moveaxis(blocks, 0, dim).reshape(shape)


def exchange_in_order(blocks, axes, sequence):
    shape = [lax.axis_size(a) for a in axes]
    blocks = blocks.reshape(*shape, *blocks.shape[1:])
    for k in sequence:
        blocks = lax.all_to_all(blocks, axes[k], split_axis=k, concat_axis=k, tiled=True)
    return blocks.reshape(-1, *blocks.shape[len(axes) :])


def exchange_by_chip(shard, groups, sequence, split_dim, concat_dim):
    devices = lax.axis_size(groups[0]) * lax.axis_size(groups[1])
    blocks = in_blocks(shard, split_dim, devices)
    return in_order(exchange_in_order(blocks, groups, sequence), concat_dim)


def head_scores(query, keys):
    factor = 1.0 / math.sqrt(query.shape[-1])
    return jnp.einsum("fahd,fbhd->fhab", query, keys, preferred_element_type=jnp.float32) * factor


def frame_attention(parts):
    query, keys, values = parts
    frames, count, heads, head_dim = query.shape
    block = math.gcd(count, 512)
    blocks = jnp.moveaxis(query.reshape(frames, count // block, block, heads, head_dim), 1, 0)

    def one_block(rows):
        scores = head_scores(rows, keys)
        top = jnp.max(scores, axis=-1, keepdims=True)
        probs = jnp.exp(scores - top)
        total = jnp.sum(probs, axis=-1)
        mixed = jnp.einsum(
            "fhab,fbhd->fahd",
            probs.astype(jnp.bfloat16),
            values,
            preferred_element_type=jnp.float32,
        )
        return (mixed / jnp.transpose(total, (0, 2, 1))[..., None]).astype(jnp.bfloat16)

    result = lax.map(one_block, blocks)
    return jnp.moveaxis(result, 0, 1).reshape(frames, count, heads, head_dim)


def temporal_mix(packed, allowed):
    frames, count = (packed.shape[0], packed.shape[1])
    width = packed.shape[2] // 3
    head_dim = width // HEADS
    split = (frames, count, HEADS, head_dim)
    query = packed[:, :, :width].reshape(split)
    keys = packed[:, :, width : 2 * width].reshape(split)
    values = packed[:, :, 2 * width :].reshape(split)
    scores = jnp.einsum("anhd,bnhd->nhab", query, keys, preferred_element_type=jnp.float32) * (
        1.0 / math.sqrt(head_dim)
    )
    scores = jnp.where(allowed, scores, neg_fill)
    top = jnp.max(scores, axis=-1, keepdims=True)
    probs = jnp.exp(scores - top)
    total = jnp.sum(probs, axis=-1)
    mixed = jnp.einsum(
        "nhab,bnhd->anhd", probs.astype(jnp.bfloat16), values, preferred_element_type=jnp.float32
    )
    mixed = mixed / jnp.transpose(total, (2, 0, 1))[..., None]
    return mixed.reshape(frames, count, width)


def shards(
    spatial_query,
    spatial_key,
    spatial_value,
    latents,
    proj_weight,
    proj_bias,
    residual_gate,
    temporal_shift,
    temporal_scale,
    temporal_weight,
    clip_lengths,
):
    frames_dev, patches_dev, width = latents.shape
    head_dim = width // HEADS
    split = (frames_dev, patches_dev, HEADS, head_dim)
    query = spatial_query.reshape(split)
    mixed_heads = frame_attention(
        (
            lax.all_to_all(query, "space", split_axis=2, concat_axis=1, tiled=True),
            lax.all_to_all(
                spatial_key.reshape(split), "space", split_axis=2, concat_axis=1, tiled=True
            ),
            lax.all_to_all(
                spatial_value.reshape(split), "space", split_axis=2, concat_axis=1, tiled=True
            ),
        )
    )
    attended = lax.all_to_all(mixed_heads, "space", split_axis=1, concat_axis=2, tiled=True)
    rows = frames_dev * patches_dev
    flat = attended.reshape(rows, width)
    projected = jnp.dot(
        flat,
        lax.all_gather(proj_weight, FRAME, axis=0, tiled=True),
        preferred_element_type=jnp.float32,
    )
    hidden = latents.reshape(rows, width).astype(jnp.float32) + residual_gate * (
        projected + proj_bias
    )
    mean = jnp.mean(hidden, axis=-1, keepdims=True)
    centred = hidden - mean
    variance = jnp.mean(centred * centred, axis=-1, keepdims=True)
    normed = (
        centred * lax.rsqrt(variance + 1e-06) * (1.0 + temporal_scale) + temporal_shift
    ).astype(jnp.bfloat16)
    groups = lax.axis_size(FRAME)
    frames_all = frames_dev * groups
    per_group = patches_dev // groups
    ends = jnp.cumsum(clip_lengths)
    clip_of = jnp.sum(
        (jnp.arange(frames_all, dtype=jnp.int32)[:, None] >= ends[None, :]).astype(jnp.int32),
        axis=1,
    )
    allowed = clip_of[:, None] == clip_of[None, :]
    whole_weight = lax.all_gather(temporal_weight, FRAME, axis=0, tiled=True)
    local = jnp.einsum(
        "fnc,ce->fne",
        exchange_by_chip(
            normed.reshape(frames_dev, groups, per_group, width),
            (("frame_0", "frame_1"), "frame_2"),
            (1, 0),
            1,
            0,
        )[:, 0],
        whole_weight,
        preferred_element_type=jnp.float32,
    ).astype(jnp.bfloat16)
    temporal = temporal_mix(local, allowed)[:, None]
    temporal = temporal.reshape(frames_all, per_group, width)
    temporal_out = lax.all_to_all(
        temporal.astype(jnp.bfloat16), FRAME, split_axis=0, concat_axis=1, tiled=True
    ).astype(temporal.dtype)
    return (hidden.reshape(frames_dev, patches_dev, width), temporal_out)


def solution(mesh):
    split = Mesh(
        mesh.devices.reshape(2, 8, 2, mesh.shape["space"]),
        ("frame_0", "frame_1", "frame_2", "space"),
    )
    return jax.shard_map(
        shards,
        mesh=split,
        in_specs=(
            P(FRAME, "space", None),
            P(FRAME, "space", None),
            P(FRAME, "space", None),
            P(FRAME, "space", None),
            P(FRAME, None),
            P(),
            P(),
            P(),
            P(),
            P(FRAME, None),
            P(),
        ),
        out_specs=(P(FRAME, "space", None), P(FRAME, "space", None)),
        check_vma=False,
    )
```

profile of v0, /device:TPU:1, one launch (start us, length us, event | category | flops | bytes accessed | tf_op | source)
XLA Modules:
  0.0 205.7 jit_solution(14141695110795643575)
XLA Ops:
  7.2 0.7 all-gather.5.cloned.1.call-update
  8.0 0.7 all-gather.7.cloned.1.call-update
  8.7 1.4 reshape.123
  10.0 0.8 copy.88
  10.8 10.2 %all-to-all-start = ((bf16[1,64,16,72]{3,1,0,2:T(8,128)(2,1)}), bf16[1,64,16,72]{3,1,0,2:T(8,128)(2,1)S(1)}, u32[]{:S(2)}, u32[]{:S(2)}) async-start(bf16[1,64,16,72]{3,1,0,2:T(8,128)(2,1)} %copy.88), calls=%async_computation | async-start | bytes 524288 | tf_op jit(solution)/shard_map/all_to_all | solution.py:107
  21.0 1.4 reshape.124
  22.4 0.8 copy.90
  23.2 10.2 %all-to-all-done = bf16[1,64,16,72]{3,1,0,2:T(8,128)(2,1)S(1)} async-done(((bf16[1,64,16,72]{3,1,0,2:T(8,128)(2,1)}), bf16[1,64,16,72]{3,1,0,2:T(8,128)(2,1)S(1)}, u32[]{:S(2)}, u32[]{:S(2)}) %all-to-all-start) | async-done | bytes 147488 | tf_op jit(solution)/shard_map/all_to_all | solution.py:107
  33.4 3.9 %all-to-all-start.1 = ((bf16[1,64,16,72]{3,1,0,2:T(8,128)(2,1)}), bf16[1,64,16,72]{3,1,0,2:T(8,128)(2,1)S(1)}, u32[]{:S(2)}, u32[]{:S(2)}) async-start(bf16[1,64,16,72]{3,1,0,2:T(8,128)(2,1)} %copy.90), calls=%async_computation.1 | async-start | bytes 524288 | tf_op jit(solution)/shard_map/all_to_all | solution.py:108
  37.7 0.8 copy.92
  38.5 13.1 %all-to-all-done.1 = bf16[1,64,16,72]{3,1,0,2:T(8,128)(2,1)S(1)} async-done(((bf16[1,64,16,72]{3,1,0,2:T(8,128)(2,1)}), bf16[1,64,16,72]{3,1,0,2:T(8,128)(2,1)S(1)}, u32[]{:S(2)}, u32[]{:S(2)}) %all-to-all-start.1) | async-done | bytes 147488 | tf_op jit(solution)/shard_map/all_to_all | solution.py:108
  51.6 3.5 %all-to-all-start.2 = ((bf16[1,64,16,72]{3,1,0,2:T(8,128)(2,1)}), bf16[1,64,16,72]{3,1,0,2:T(8,128)(2,1)S(1)}, u32[]{:S(2)}, u32[]{:S(2)}) async-start(bf16[1,64,16,72]{3,1,0,2:T(8,128)(2,1)} %copy.92), calls=%async_computation.2 | async-start | bytes 524288 | tf_op jit(solution)/shard_map/all_to_all | solution.py:111
  55.4 14.1 %all-to-all-done.2 = bf16[1,64,16,72]{3,1,0,2:T(8,128)(2,1)S(1)} async-done(((bf16[1,64,16,72]{3,1,0,2:T(8,128)(2,1)}), bf16[1,64,16,72]{3,1,0,2:T(8,128)(2,1)S(1)}, u32[]{:S(2)}, u32[]{:S(2)}) %all-to-all-start.2) | async-done | bytes 147488 | tf_op jit(solution)/shard_map/all_to_all | solution.py:111
  69.7 3.4 %while.10 = (s32[]{:T(128)}, bf16[2,1,512,1,72]{2,4,3,1,0:T(8,128)(2,1)S(1)}, bf16[2,1,512,1,72]{2,4,3,1,0:T(8,128)(2,1)S(1)}, bf16[1,1024,1,72]{1,3,2,0:T(8,128...) while((s32[]{:T(128)}, bf16[2,1,512,1,72]{2,4,3,1,0:T(8,128)(2,1)S(1)}, ...), condition=%wide.region_3.4_spmd, body=%wide.region_0.3_spmd.sunk | while | flops 155261952 | bytes 6744149 | solution.py:62
  69.7 0.6 multiply_reduce_fusion.3
  70.8 0.6 fusion.40
  72.5 0.6 fusion.40
  73.9 2.3 %reduce.5 = bf16[1024,72]{1,0:T(8,128)(2,1)S(1)} reduce(bf16[1024,1,1,72]{3,2,1,0:T(2,128)(2,1)S(1)} %bitcast.98, bf16[]{:T(256)} %broadcast.46), dimensions={1,2}, to_apply=%bitcast.78.reduce_sub_computation | reduce | bytes 294914
  76.2 1.2 reshape.144
  77.4 3.5 %all-to-all-start.3 = ((bf16[16,2,2304]{2,1,0:T(2,128)(2,1)}), bf16[16,2,2304]{2,1,0:T(2,128)(2,1)S(1)}, u32[]{:S(2)}, u32[]{:S(2)}) async-start(bf16[16,2,2304]{2,1,0:T(2,128)(2,1)} %reshape.144), calls=%async_computation.3 | async-start | bytes 294912 | tf_op jit(solution)/shard_map/all_to_all | solution.py:116
  81.2 9.5 %all-to-all-done.3 = bf16[16,2,2304]{2,1,0:T(2,128)(2,1)S(1)} async-done(((bf16[16,2,2304]{2,1,0:T(2,128)(2,1)}), bf16[16,2,2304]{2,1,0:T(2,128)(2,1)S(1)}, u32[]{:S(2)}, u32[]{:S(2)}) %all-to-all-start.3) | async-done | bytes 147488 | tf_op jit(solution)/shard_map/all_to_all | solution.py:116
  90.7 0.9 reshape.145
  92.9 3.6 %reshape.136 = bf16[1152,1152]{1,0:T(8,128)(2,1)S(1)} reshape(bf16[32,36,1152]{2,1,0:T(8,128)(2,1)} %all-gather.5.cloned.1.call-done) | data formatting | bytes 5308416
  96.6 0.7 fusion.28
  97.8 6.7 %all_to_all.85 = bf16[16,2,1,1,2,1152]{5,4,0,3,2,1:T(2,128)(2,1)S(1)} all-to-all(bf16[16,2,1,1,2,1152]{5,4,0,3,2,1:T(2,128)(2,1)S(1)} %copy.99), channel_id=1, replica_groups=mesh['frame_0'=2,'frame_1'=8,'frame_2'=2,'space'=16] {'frame_2'}, dimensions={1} | all-to-all | bytes 294912 | tf_op jit(solution)/shard_map/all_to_all | solution.py:28
  104.5 0.8 copy.100
  105.3 9.1 %all-to-all-start.5 = ((bf16[16,2,1,1,2,1152]{5,4,1,3,2,0:T(2,128)(2,1)}), bf16[16,2,1,1,2,1152]{5,4,1,3,2,0:T(2,128)(2,1)S(1)}, u32[]{:S(2)}, u32[]{:S(2)}) async-start(bf16[16,2,1,1,2,1152]{5,4,1,3,2,0:T(2,128)(2,1)} %copy.100), calls=%async_computation.5 | async-start | bytes 294912 | tf_op jit(solution)/shard_map/all_to_all | solution.py:28
  114.6 49.2 %all-gather.7.cloned.1.call-done = bf16[32,36,3456]{2,1,0:T(8,128)(2,1)} async-done(((bf16[1,36,3456]{2,1,0:T(8,128)(2,1)}), bf16[32,36,3456]{2,1,0:T(8,128)(2,1)}) %all-gather.7.cloned.1.call-update) | async-done | bytes 7962640 | tf_op jit(solution)/shard_map/all_gather | solution.py:142
  163.8 12.4 %reshape.139 = bf16[1152,3456,1]{1,0,2:T(8,128)(2,1)} reshape(bf16[32,36,3456]{2,1,0:T(8,128)(2,1)} %all-gather.7.cloned.1.call-done) | data formatting | bytes 15925248
  176.2 4.6 %convolution_convert_fusion = bf16[32,2,3456]{2,0,1:T(8,128)(2,1)S(1)} fusion(bf16[1152,3456,1]{1,0,2:T(8,128)(2,1)} %reshape.139, bf16[32,2,1152]{2,1,0:T(2,128)(2,1)S(1)} %bitcast.104), kind=kOutput, calls=%fused_computation.16 | convolution fusion | flops 509829120 | bytes 8552448 | tf_op jit(solution)/shard_map/fnc,ce->fne/dot_general | solution.py:143
  183.5 14.6 %all_to_all.86 = bf16[32,2,1152]{2,1,0:T(2,128)(2,1)S(1)} all-to-all(bf16[32,2,1152]{2,1,0:T(2,128)(2,1)S(1)} %reshape.142), channel_id=1, replica_groups=mesh['frame_0'=2,'frame_1'=8,'frame_2'=2,'space'=16] {'frame_0','frame_1..., dimensions={0} | all-to-all | bytes 294912 | tf_op jit(solution)/shard_map/all_to_all | solution.py:157
  198.1 0.8 reshape.134
  (56 shorter events, 8.2 us)
Async XLA Ops:
  7.2 30.1 %copy-start.1 = (bf16[1,64,1152]{2,1,0:T(8,128)(2,1)S(1)}, bf16[1,64,1152]{2,1,0:T(8,128)(2,1)}, u32[]{:S(2)}) copy-start(bf16[1,64,1152]{2,1,0:T(8,128)(2,1)} %param.15) | copy-start | bytes 442372
  7.2 85.7 %all-gather.5.cloned.1.call-start = ((), (), s32[]{:S(2)}) async-start(), calls=%async_computation.7 | async-start | bytes 3041280 | tf_op jit(solution)/shard_map/all_gather | solution.py:121
  7.9 155.8 %all-gather.7.cloned.1.call-start = ((), (), s32[]{:S(2)}) async-start(), calls=%async_computation.8 | async-start | bytes 9123840 | tf_op jit(solution)/shard_map/all_gather | solution.py:142
  10.8 22.6 %all-to-all-start = ((bf16[1,64,16,72]{3,1,0,2:T(8,128)(2,1)}), bf16[1,64,16,72]{3,1,0,2:T(8,128)(2,1)S(1)}, u32[]{:S(2)}, u32[]{:S(2)}) async-start(bf16[1,64,16,72]{3,1,0,2:T(8,128)(2,1)} %copy.88), calls=%async_computation | async-start | bytes 524288 | tf_op jit(solution)/shard_map/all_to_all | solution.py:107
  33.4 18.2 %all-to-all-start.1 = ((bf16[1,64,16,72]{3,1,0,2:T(8,128)(2,1)}), bf16[1,64,16,72]{3,1,0,2:T(8,128)(2,1)S(1)}, u32[]{:S(2)}, u32[]{:S(2)}) async-start(bf16[1,64,16,72]{3,1,0,2:T(8,128)(2,1)} %copy.90), calls=%async_computation.1 | async-start | bytes 524288 | tf_op jit(solution)/shard_map/all_to_all | solution.py:108
  51.6 18.0 %all-to-all-start.2 = ((bf16[1,64,16,72]{3,1,0,2:T(8,128)(2,1)}), bf16[1,64,16,72]{3,1,0,2:T(8,128)(2,1)S(1)}, u32[]{:S(2)}, u32[]{:S(2)}) async-start(bf16[1,64,16,72]{3,1,0,2:T(8,128)(2,1)} %copy.92), calls=%async_computation.2 | async-start | bytes 524288 | tf_op jit(solution)/shard_map/all_to_all | solution.py:111
  73.1 7.8 %copy-start.7 = (s32[16]{0:T(128)S(1)}, s32[16]{0:T(128)}, u32[]{:S(2)}) copy-start(s32[16]{0:T(128)} %param.23) | copy-start | bytes 196
  73.1 8.1 %copy-start.6 = (f32[1152]{0:T(1024)S(1)}, f32[1152]{0:T(1024)}, u32[]{:S(2)}) copy-start(f32[1152]{0:T(1024)} %param.21) | copy-start | bytes 13828
  77.4 13.3 %all-to-all-start.3 = ((bf16[16,2,2304]{2,1,0:T(2,128)(2,1)}), bf16[16,2,2304]{2,1,0:T(2,128)(2,1)S(1)}, u32[]{:S(2)}, u32[]{:S(2)}) async-start(bf16[16,2,2304]{2,1,0:T(2,128)(2,1)} %reshape.144), calls=%async_computation.3 | async-start | bytes 294912 | tf_op jit(solution)/shard_map/all_to_all | solution.py:116
  92.8 3.7 %copy-start.2 = (bf16[1,64,1152]{2,1,0:T(8,128)(2,1)S(1)}, bf16[1,64,1152]{2,1,0:T(8,128)(2,1)}, u32[]{:S(2)}) copy-start(bf16[1,64,1152]{2,1,0:T(8,128)(2,1)} %param.16) | copy-start | bytes 442372
  92.9 3.7 %copy-start.3 = (f32[1152]{0:T(1024)S(1)}, f32[1152]{0:T(1024)}, u32[]{:S(2)}) copy-start(f32[1152]{0:T(1024)} %param.18) | copy-start | bytes 13828
  92.9 3.7 %copy-start.4 = (f32[1152]{0:T(1024)S(1)}, f32[1152]{0:T(1024)}, u32[]{:S(2)}) copy-start(f32[1152]{0:T(1024)} %param.19) | copy-start | bytes 13828
  96.6 0.9 copy-start.5
  97.3 78.9 %copy-start = (f32[64,1152]{1,0:T(8,128)}, f32[64,1152]{1,0:T(8,128)S(1)}, u32[]{:S(2)}) copy-start(f32[64,1152]{1,0:T(8,128)S(1)} %get-tuple-element.71) | copy-start | bytes 884740
  105.3 70.9 %all-to-all-start.5 = ((bf16[16,2,1,1,2,1152]{5,4,1,3,2,0:T(2,128)(2,1)}), bf16[16,2,1,1,2,1152]{5,4,1,3,2,0:T(2,128)(2,1)S(1)}, u32[]{:S(2)}, u32[]{:S(2)}) async-start(bf16[16,2,1,1,2,1152]{5,4,1,3,2,0:T(2,128)(2,1)} %copy.100), calls=%async_computation.5 | async-start | bytes 294912 | tf_op jit(solution)/shard_map/all_to_all | solution.py:28
Sparse Core Ops, SparseCore 0:
  10.1 74.3 all-gather.4
  86.6 77.0 all-gather.6
where the time goes:
time: 207 us; the launch traced here: 206 us
  waiting for transfers between devices  97.6 us (47%)
  starting transfers between devices  30.3 us (15%)
  local copies, waits for them, and re-layouts  29.8 us (14%)
  blocking collectives  21.3 us (10%)
  between operations  14.4 us (7%)
  matrix products  8.13 us (4%)
  other arithmetic  4.11 us (2%)
    all_gather x1, waiting for transfers between devices, shards(): whole_weight = lax.all_gather(temporal_weight, FRAME, axis=0, tiled=True)  49.2 us
    unnamed x21, local copies, waits for them, and re-layouts  18.7 us
    all_to_all x1, blocking collectives, shards(): lax.all_to_all(temporal.astype(jnp.bfloat16), FRAME, split_axis=0, concat...  14.6 us
    all_to_all x1, waiting for transfers between devices, shards(): lax.all_to_all(spatial_value.reshape(split), 'space', split_axis=2, conca...  14.1 us
    all_to_all x1, waiting for transfers between devices, shards(): lax.all_to_all(spatial_key.reshape(split), 'space', split_axis=2, concat_...  13.1 us
    all_to_all x1, starting transfers between devices, shards(): lax.all_to_all(query, 'space', split_axis=2, concat_axis=1, tiled=True)  10.2 us
    all_to_all x1, waiting for transfers between devices, shards(): lax.all_to_all(query, 'space', split_axis=2, concat_axis=1, tiled=True)  10.2 us
    all_to_all x1, waiting for transfers between devices, shards(): lax.all_to_all(mixed_heads, 'space', split_axis=1, concat_axis=2, tiled=T...  9.53 us
  transfers between devices with their start and end apart: 7, of which 5 were waited for; matrix products, arithmetic and copies ran while one was open for 16% of the time, Pallas kernels for 0%

commit v1 on v0

--- a/solution.py
+++ b/solution.py
@@ -139,7 +139,10 @@
         axis=1,
     )
     allowed = clip_of[:, None] == clip_of[None, :]
-    whole_weight = lax.all_gather(temporal_weight, FRAME, axis=0, tiled=True)
+    size = lax.axis_size(FRAME)
+    pieces = jnp.stack([temporal_weight for _ in range(size)])
+    pieces = lax.all_to_all(pieces, FRAME, split_axis=0, concat_axis=0)
+    whole_weight = jnp.concatenate(pieces, axis=0)
     local = jnp.einsum(
         "fnc,ce->fne",
         exchange_by_chip(

time: 207 us -> 382 us (1.85)
  waiting for transfers between devices: 97.6 us -> 253 us
  starting transfers between devices: 30.3 us -> 43.7 us
  local copies, waits for them, and re-layouts: 29.8 us -> 33.8 us
    all_to_all x0 -> x1, waiting for transfers between devices: none -> 205 us  [shards(): pieces = lax.all_to_all(pieces, FRAME, split_axis=0, concat_axis=0)]
    all_gather x1 -> x0, waiting for transfers between devices: 49.2 us -> none  [shards(): whole_weight = lax.all_gather(temporal_weight, FRAME, axis=0, tiled=True)]
    reshape x0 -> x1, local copies, waits for them, and re-layouts: none -> 12.4 us  [shards(): whole_weight = jnp.concatenate(pieces, axis=0)]
    unnamed x21 -> x22, local copies, waits for them, and re-layouts: 18.7 us -> 6.26 us
    all_to_all x0 -> x1, starting transfers between devices: none -> 11.2 us  [shards(): pieces = lax.all_to_all(pieces, FRAME, split_axis=0, concat_axis=0)]
    another operation x1 -> x2, local copies, waits for them, and re-layouts: 0.08 us -> 4.09 us  [the longest x1 4 us: shards(): pieces = jnp.stack([temporal_weight for _ in range(size)])]
  transfers between devices with their start and end apart: 7 -> 7, of which waited for: 5 -> 5; matrix products, arithmetic and copies ran while one was open for 16% -> 8% of each run, Pallas kernels for 0% -> 0%
where the time goes in v1:
time: 382 us; the launch traced here: 381 us
  waiting for transfers between devices  253 us (66%)
  starting transfers between devices  43.7 us (11%)
  local copies, waits for them, and re-layouts  33.8 us (9%)
  blocking collectives  23.8 us (6%)
  between operations  14.4 us (4%)
  matrix products  8.13 us (2%)
  other arithmetic  4.11 us (1%)
    all_to_all x1, waiting for transfers between devices, shards(): pieces = lax.all_to_all(pieces, FRAME, split_axis=0, concat_axis=0)  205 us
    all_to_all x1, blocking collectives, shards(): lax.all_to_all(temporal.astype(jnp.bfloat16), FRAME, split_axis=0, concat...  17.5 us
    all_to_all x1, waiting for transfers between devices, shards(): lax.all_to_all(spatial_value.reshape(split), 'space', split_axis=2, conca...  14.4 us
    all_to_all x1, waiting for transfers between devices, shards(): lax.all_to_all(spatial_key.reshape(split), 'space', split_axis=2, concat_...  12.5 us
    reshape x1, local copies, waits for them, and re-layouts, shards(): whole_weight = jnp.concatenate(pieces, axis=0)  12.4 us
    all_to_all x1, starting transfers between devices, exchange_in_order(): lax.all_to_all(blocks, axes[k], split_axis=k, concat_axis=k, tiled=True)  11.3 us
    all_to_all x1, starting transfers between devices, shards(): pieces = lax.all_to_all(pieces, FRAME, split_axis=0, concat_axis=0)  11.2 us
    all_to_all x1, starting transfers between devices, shards(): lax.all_to_all(query, 'space', split_axis=2, concat_axis=1, tiled=True)  10.2 us
  transfers between devices with their start and end apart: 7, of which 5 were waited for; matrix products, arithmetic and copies ran while one was open for 8% of the time, Pallas kernels for 0%

profile of v1, /device:TPU:1, one launch (start us, length us, event | category | flops | bytes accessed | tf_op | source)
XLA Modules:
  0.0 380.6 jit_solution(4945488893608150947)
XLA Ops:
  7.2 0.7 all-gather.3.cloned.1.call-update
  7.9 1.4 reshape.128
  9.3 0.8 copy.88
  10.1 10.2 %all-to-all-start = ((bf16[1,64,16,72]{3,1,0,2:T(8,128)(2,1)}), bf16[1,64,16,72]{3,1,0,2:T(8,128)(2,1)S(1)}, u32[]{:S(2)}, u32[]{:S(2)}) async-start(bf16[1,64,16,72]{3,1,0,2:T(8,128)(2,1)} %copy.88), calls=%async_computation | async-start | bytes 524288 | tf_op jit(solution)/shard_map/all_to_all | solution.py:107
  20.3 1.4 reshape.129
  21.7 0.8 copy.90
  22.4 10.2 %all-to-all-done = bf16[1,64,16,72]{3,1,0,2:T(8,128)(2,1)S(1)} async-done(((bf16[1,64,16,72]{3,1,0,2:T(8,128)(2,1)}), bf16[1,64,16,72]{3,1,0,2:T(8,128)(2,1)S(1)}, u32[]{:S(2)}, u32[]{:S(2)}) %all-to-all-start) | async-done | bytes 147488 | tf_op jit(solution)/shard_map/all_to_all | solution.py:107
  32.6 3.9 %all-to-all-start.1 = ((bf16[1,64,16,72]{3,1,0,2:T(8,128)(2,1)}), bf16[1,64,16,72]{3,1,0,2:T(8,128)(2,1)S(1)}, u32[]{:S(2)}, u32[]{:S(2)}) async-start(bf16[1,64,16,72]{3,1,0,2:T(8,128)(2,1)} %copy.90), calls=%async_computation.1 | async-start | bytes 524288 | tf_op jit(solution)/shard_map/all_to_all | solution.py:108
  37.0 0.8 copy.92
  37.8 12.5 %all-to-all-done.1 = bf16[1,64,16,72]{3,1,0,2:T(8,128)(2,1)S(1)} async-done(((bf16[1,64,16,72]{3,1,0,2:T(8,128)(2,1)}), bf16[1,64,16,72]{3,1,0,2:T(8,128)(2,1)S(1)}, u32[]{:S(2)}, u32[]{:S(2)}) %all-to-all-start.1) | async-done | bytes 147488 | tf_op jit(solution)/shard_map/all_to_all | solution.py:108
  50.3 3.5 all-to-all-start.2
  54.1 14.4 %all-to-all-done.2 = bf16[1,64,16,72]{3,1,0,2:T(8,128)(2,1)S(1)} async-done(((bf16[1,64,16,72]{3,1,0,2:T(8,128)(2,1)}), bf16[1,64,16,72]{3,1,0,2:T(8,128)(2,1)S(1)}, u32[]{:S(2)}, u32[]{:S(2)}) %all-to-all-start.2) | async-done | bytes 147488 | tf_op jit(solution)/shard_map/all_to_all | solution.py:111
  68.6 3.4 while.10
  69.7 0.6 fusion.40
  71.4 0.6 fusion.40
  72.8 2.3 reduce.5
  75.1 1.2 reshape.148
  76.3 3.5 all-to-all-start.3
  79.8 9.8 %all-to-all-done.3 = bf16[16,2,2304]{2,1,0:T(2,128)(2,1)S(1)} async-done(((bf16[16,2,2304]{2,1,0:T(2,128)(2,1)}), bf16[16,2,2304]{2,1,0:T(2,128)(2,1)S(1)}, u32[]{:S(2)}, u32[]{:S(2)}) %all-to-all-start.3) | async-done | bytes 147488 | tf_op jit(solution)/shard_map/all_to_all | solution.py:116
  89.6 0.9 reshape.149
  91.8 3.6 reshape.142
  95.5 0.7 fusion.28
  96.8 6.3 %all_to_all.90 = bf16[16,2,1,1,2,1152]{5,4,0,3,2,1:T(2,128)(2,1)S(1)} all-to-all(bf16[16,2,1,1,2,1152]{5,4,0,3,2,1:T(2,128)(2,1)S(1)} %copy.99), channel_id=1, replica_groups=mesh['frame_0'=2,'frame_1'=8,'frame_2'=2,'space'=16] {'frame_2'}, dimensions={1} | all-to-all | bytes 294912 | tf_op jit(solution)/shard_map/all_to_all | solution.py:28
  103.0 4.0 %stack.2 = bf16[32,36,3456]{2,1,0:T(8,128)(2,1)} broadcast(bf16[36,3456]{1,0:T(8,128)(2,1)S(1)} %copy-done.1), dimensions={1,2} | broadcast | bytes 8211456 | tf_op jit(solution)/shard_map/stack | solution.py:143
  107.1 11.2 %all-to-all-start.6 = ((bf16[32,36,3456]{2,1,0:T(8,128)(2,1)}), bf16[32,36,3456]{2,1,0:T(8,128)(2,1)}, u32[]{:S(2)}, u32[]{:S(2)}) async-start(bf16[32,36,3456]{2,1,0:T(8,128)(2,1)} %stack.2), calls=%async_computation.6 | async-start | bytes 17694720 | tf_op jit(solution)/shard_map/all_to_all | solution.py:144
  118.6 0.8 copy.100
  119.3 204.9 %all-to-all-done.6 = bf16[32,36,3456]{2,1,0:T(8,128)(2,1)} async-done(((bf16[32,36,3456]{2,1,0:T(8,128)(2,1)}), bf16[32,36,3456]{2,1,0:T(8,128)(2,1)}, u32[]{:S(2)}, u32[]{:S(2)}) %all-to-all-start.6) | async-done | bytes 7962656 | tf_op jit(solution)/shard_map/all_to_all | solution.py:144
  324.2 11.3 %all-to-all-start.5 = ((bf16[16,2,1,1,2,1152]{5,4,1,3,2,0:T(2,128)(2,1)}), bf16[16,2,1,1,2,1152]{5,4,1,3,2,0:T(2,128)(2,1)S(1)}, u32[]{:S(2)}, u32[]{:S(2)}) async-start(bf16[16,2,1,1,2,1152]{5,4,1,3,2,0:T(2,128)(2,1)} %copy.100), calls=%async_computation.5 | async-start | bytes 294912 | tf_op jit(solution)/shard_map/all_to_all | solution.py:28
  335.7 12.4 %reshape.143 = bf16[1152,3456,1]{1,0,2:T(8,128)(2,1)} reshape(bf16[32,36,3456]{2,1,0:T(8,128)(2,1)} %all-to-all-done.6) | data formatting | bytes 15925248 | tf_op jit(solution)/shard_map/reshape | solution.py:145
  348.1 4.6 %convolution_convert_fusion = bf16[32,2,3456]{2,0,1:T(8,128)(2,1)S(1)} fusion(bf16[1152,3456,1]{1,0,2:T(8,128)(2,1)} %reshape.143, bf16[32,2,1152]{2,1,0:T(2,128)(2,1)S(1)} %bitcast.103), kind=kOutput, calls=%fused_computation.16 | convolution fusion | flops 509829120 | bytes 8552448 | tf_op jit(solution)/shard_map/fnc,ce->fne/dot_general | solution.py:146
  355.5 17.5 %all_to_all.91 = bf16[32,2,1152]{2,1,0:T(2,128)(2,1)S(1)} all-to-all(bf16[32,2,1152]{2,1,0:T(2,128)(2,1)S(1)} %reshape.146), channel_id=1, replica_groups=mesh['frame_0'=2,'frame_1'=8,'frame_2'=2,'space'=16] {'frame_0','frame_1..., dimensions={0} | all-to-all | bytes 294912 | tf_op jit(solution)/shard_map/all_to_all | solution.py:160
  373.0 0.8 reshape.140
  (58 shorter events, 8.7 us)
Async XLA Ops:
  7.2 29.3 %copy-start.2 = (bf16[1,64,1152]{2,1,0:T(8,128)(2,1)S(1)}, bf16[1,64,1152]{2,1,0:T(8,128)(2,1)}, u32[]{:S(2)}) copy-start(bf16[1,64,1152]{2,1,0:T(8,128)(2,1)} %param.15) | copy-start | bytes 442372
  7.2 84.7 %all-gather.3.cloned.1.call-start = ((), (), s32[]{:S(2)}) async-start(), calls=%async_computation.8 | async-start | bytes 3041280 | tf_op jit(solution)/shard_map/all_gather | solution.py:121
  10.1 22.6 %all-to-all-start = ((bf16[1,64,16,72]{3,1,0,2:T(8,128)(2,1)}), bf16[1,64,16,72]{3,1,0,2:T(8,128)(2,1)S(1)}, u32[]{:S(2)}, u32[]{:S(2)}) async-start(bf16[1,64,16,72]{3,1,0,2:T(8,128)(2,1)} %copy.88), calls=%async_computation | async-start | bytes 524288 | tf_op jit(solution)/shard_map/all_to_all | solution.py:107
  32.6 17.6 %all-to-all-start.1 = ((bf16[1,64,16,72]{3,1,0,2:T(8,128)(2,1)}), bf16[1,64,16,72]{3,1,0,2:T(8,128)(2,1)S(1)}, u32[]{:S(2)}, u32[]{:S(2)}) async-start(bf16[1,64,16,72]{3,1,0,2:T(8,128)(2,1)} %copy.90), calls=%async_computation.1 | async-start | bytes 524288 | tf_op jit(solution)/shard_map/all_to_all | solution.py:108
  50.3 18.2 %all-to-all-start.2 = ((bf16[1,64,16,72]{3,1,0,2:T(8,128)(2,1)}), bf16[1,64,16,72]{3,1,0,2:T(8,128)(2,1)S(1)}, u32[]{:S(2)}, u32[]{:S(2)}) async-start(bf16[1,64,16,72]{3,1,0,2:T(8,128)(2,1)} %copy.92), calls=%async_computation.2 | async-start | bytes 524288 | tf_op jit(solution)/shard_map/all_to_all | solution.py:111
  71.9 7.8 %copy-start.7 = (f32[1152]{0:T(1024)S(1)}, f32[1152]{0:T(1024)}, u32[]{:S(2)}) copy-start(f32[1152]{0:T(1024)} %param.21) | copy-start | bytes 13828
  76.3 13.4 %all-to-all-start.3 = ((bf16[16,2,2304]{2,1,0:T(2,128)(2,1)}), bf16[16,2,2304]{2,1,0:T(2,128)(2,1)S(1)}, u32[]{:S(2)}, u32[]{:S(2)}) async-start(bf16[16,2,2304]{2,1,0:T(2,128)(2,1)} %reshape.148), calls=%async_computation.3 | async-start | bytes 294912 | tf_op jit(solution)/shard_map/all_to_all | solution.py:116
  91.8 3.7 copy-start.3
  91.8 3.7 copy-start.4
  91.8 3.7 copy-start.5
  95.5 0.9 copy-start.6
  95.5 7.5 %copy-start.1 = (bf16[36,3456]{1,0:T(8,128)(2,1)S(1)}, bf16[36,3456]{1,0:T(8,128)(2,1)}, u32[]{:S(2)}) copy-start(bf16[36,3456]{1,0:T(8,128)(2,1)} %param.22) | copy-start | bytes 746500
  96.2 10.8 %copy-start = (f32[64,1152]{1,0:T(8,128)}, f32[64,1152]{1,0:T(8,128)S(1)}, u32[]{:S(2)}) copy-start(f32[64,1152]{1,0:T(8,128)S(1)} %get-tuple-element.71) | copy-start | bytes 884740
  107.1 11.3 %copy-start.8 = (s32[16]{0:T(128)S(1)}, s32[16]{0:T(128)}, u32[]{:S(2)}) copy-start(s32[16]{0:T(128)} %param.23) | copy-start | bytes 196
  107.1 217.2 %all-to-all-start.6 = ((bf16[32,36,3456]{2,1,0:T(8,128)(2,1)}), bf16[32,36,3456]{2,1,0:T(8,128)(2,1)}, u32[]{:S(2)}, u32[]{:S(2)}) async-start(bf16[32,36,3456]{2,1,0:T(8,128)(2,1)} %stack.2), calls=%async_computation.6 | async-start | bytes 17694720 | tf_op jit(solution)/shard_map/all_to_all | solution.py:144
  324.2 23.9 %all-to-all-start.5 = ((bf16[16,2,1,1,2,1152]{5,4,1,3,2,0:T(2,128)(2,1)}), bf16[16,2,1,1,2,1152]{5,4,1,3,2,0:T(2,128)(2,1)S(1)}, u32[]{:S(2)}, u32[]{:S(2)}) async-start(bf16[16,2,1,1,2,1152]{5,4,1,3,2,0:T(2,128)(2,1)} %copy.100), calls=%async_computation.5 | async-start | bytes 294912 | tf_op jit(solution)/shard_map/all_to_all | solution.py:28
Sparse Core Ops, SparseCore 0:
  10.1 74.1 all-gather.2
